TPU v7x, 32 devices: a whole 2x2x4 slice. The times are simulated.
32 devices in a mesh: shard: 8 (over y, x, core), model: 4 (over z).
Axes of the slice: x: 2, y: 2, z: 4, core: 2. Of those that a mesh axis runs over, the one named last changes fastest.
Arguments:
- weight_gate: float32 [3072, 8192], P('shard', 'model'), may hold values from -0.15625 to 0.15625
- smooth_gate: float32 [3072, 8192], P('shard', 'model'), may hold values from -0.109375 to 0.109375
- weight_up: float32 [3072, 8192], P('shard', 'model'), may hold values from -0.15625 to 0.15625
- smooth_up: float32 [3072, 8192], P('shard', 'model'), may hold values from -0.109375 to 0.109375
- norm_train: float32 [3072], P(('shard', 'model')), may hold values from 0.25 to 1.75
- norm_step: float32 [3072], P(('shard', 'model')), may hold values from -0.3 to 0.3
Outputs:
- serving_gate: bfloat16 [3072, 8192], P(None, 'model')
- serving_up: bfloat16 [3072, 8192], P(None, 'model')
- factor_gate: float32 [8192], P('model')
- factor_up: float32 [8192], P('model')
- serve_norm: bfloat16 [3072], replicated
- whole_gate: float32 [3072, 8192], P('shard', 'model')
- whole_up: float32 [3072, 8192], P('shard', 'model')
All inputs are finite; a program needn't handle non-finite values. Where the computation divides by a largest or mean magnitude, that divisor is 1e-20 or more.
Results may differ from a plain program's by a relative error of at most 0.001.
Values may be sent and summed in bfloat16 or wider, within the bound.
A program may use at most 128 MiB of HBM per device.

v0:
```python
import jax
import jax.numpy as jnp
from jax import lax
from jax.sharding import PartitionSpec as P

keep_rate = 0.7


def body(weight_gate, smooth_gate, weight_up, smooth_up, norm_train, norm_step):
    whole_gate = keep_rate * smooth_gate + (1.0 - keep_rate) * weight_gate
    whole_up = keep_rate * smooth_up + (1.0 - keep_rate) * weight_up
    factor_gate, factor_up = lax.pmax(
        (jnp.max(jnp.abs(whole_gate), axis=0), jnp.max(jnp.abs(whole_up), axis=0)), "shard"
    )
    narrow_gate, narrow_up = (
        (whole_gate / factor_gate).astype(jnp.bfloat16),
        (whole_up / factor_up).astype(jnp.bfloat16),
    )
    serving_gate, serving_up = (
        lax.all_gather(narrow_gate, "shard", axis=0, tiled=True),
        lax.all_gather(narrow_up, "shard", axis=0, tiled=True),
    )
    serve_norm = lax.all_gather(
        (norm_train + norm_step).astype(jnp.bfloat16), ("shard", "model"), axis=0, tiled=True
    )
    return (serving_gate, serving_up, factor_gate, factor_up, serve_norm, whole_gate, whole_up)


def solution(mesh):
    in_specs = (
        P("shard", "model"),
        P("shard", "model"),
        P("shard", "model"),
        P("shard", "model"),
        P(("shard", "model")),
        P(("shard", "model")),
    )
    out_specs = (
        P(None, "model"),
        P(None, "model"),
        P("model"),
        P("model"),
        P(),
        P("shard", "model"),
        P("shard", "model"),
    )
    return jax.shard_map(body, mesh=mesh, in_specs=in_specs, out_specs=out_specs, check_vma=False)
```

profile of v0, /device:TPU:0, one launch (start us, length us, event | category | flops | bytes accessed | tf_op | source)
XLA Modules:
  0.0 213.1 jit_solution(10043136426590637802)
XLA Ops:
  7.2 0.0 all-gather.5.cloned.1.call-start
  7.2 7.4 %abs_reduce_fusion = (f32[2048]{0:T(1024)S(1)}, f32[384,2048]{1,0:T(8,128)S(1)}, f32[2048]{0:T(1024)S(1)}, f32[384,2048]{1,0:T(8,128)}) fusion(f32[384,2048]{1,0:T(8,128)} %param.8, f32[384,2048]{1,0:T(8,128)} %param.9, f32[384,2048]{1,0:T(8,128)} %param.6, f32[384,2048]{1,0:T(8,128)} %param.7), kind=kLoop, calls=%fused_computation.1 | loop fusion | flops 7860224 | bytes 18890752 | tf_op jit(solution)/shard_map/reduce_max | solution.py:13
  14.6 0.0 copy-start.1
  14.6 25.5 %all-reduce.1 = (f32[2048]{0:T(1024)S(1)}, f32[2048]{0:T(1024)S(1)}) all-reduce(f32[2048]{0:T(1024)S(1)} %get-tuple-element.13, f32[2048]{0:T(1024)S(1)} %get-tuple-element.9), channel_id=1, replica_groups=mesh['shard'=8,'model'=4] {'shard'}, use_global_device_ids=true, to_apply=%region_1.0 | all-reduce | flops 4096 | bytes 32768 | tf_op jit(solution)/shard_map/pmax | solution.py:12
  40.1 0.0 copy-start.3
  40.1 0.0 copy-start.2
  40.1 1.5 divide_convert_fusion
  41.6 0.0 all-gather.5.cloned.1.call-update
  41.6 0.0 copy-done.1
  41.6 0.0 copy-done.3
  41.6 0.0 all-gather.3.cloned.1.call-start
  41.7 0.0 copy-done.2
  41.7 0.0 copy-start.4
  41.7 0.0 copy-start.5
  41.7 3.4 %divide_convert_fusion.1 = bf16[384,2048]{1,0:T(8,128)(2,1)} fusion(f32[384,2048]{1,0:T(8,128)} %get-tuple-element.27, f32[2048]{0:T(1024)S(1)} %get-tuple-element.24), kind=kLoop, calls=%fused_computation.3 | loop fusion | flops 1572864 | bytes 4726784 | tf_op jit(solution)/shard_map/convert_element_type | solution.py:16
  45.1 0.0 all-gather.3.cloned.1.call-update
  45.1 0.0 copy-done.4
  45.1 0.0 copy-done.5
  45.2 0.2 dynamic-update-slice
  45.4 40.7 %all-reduce = bf16[3072]{0:T(1024)(128)(2,1)} all-reduce(bf16[3072]{0:T(1024)(128)(2,1)S(1)} %dynamic-update-slice), channel_id=1, replica_groups=mesh['shard'=8,'model'=4] {'shard','model'}, use_global_device_ids=true, to_apply=%add | all-reduce | flops 3072 | bytes 12288
  86.1 28.0 %all-gather.5.cloned.1.call-done = bf16[3072,2048]{1,0:T(8,128)(2,1)} async-done(((bf16[384,2048]{1,0:T(8,128)(2,1)}), bf16[3072,2048]{1,0:T(8,128)(2,1)}) %all-gather.5.cloned.1.call-update) | async-done | bytes 12582928 | tf_op jit(solution)/shard_map/all_gather | solution.py:21
  114.1 74.5 %all-gather.3.cloned.1.call-done = bf16[3072,2048]{1,0:T(8,128)(2,1)} async-done(((bf16[384,2048]{1,0:T(8,128)(2,1)}), bf16[3072,2048]{1,0:T(8,128)(2,1)}) %all-gather.3.cloned.1.call-update) | async-done | bytes 12582928 | tf_op jit(solution)/shard_map/all_gather | solution.py:20
  188.6 0.0 copy-start
  188.6 11.4 %copy.16 = bf16[3072,2048]{1,0:T(8,128)(2,1)} copy(bf16[3072,2048]{1,0:T(8,128)(2,1)} %all-gather.3.cloned.1.call-done) | data formatting | bytes 25165824
  199.9 1.5 copy-done
  201.5 4.8 %copy.17 = bf16[3072,2048]{1,0:T(8,128)(2,1)} copy(bf16[3072,2048]{1,0:T(8,128)(2,1)S(1)} %copy-done) | data formatting | bytes 25165824
  (2 shorter events, 0.0 us)
Async XLA Ops:
  7.2 106.9 %all-gather.5.cloned.1.call-start = ((), (), s32[]{:S(2)}) async-start(), calls=%async_computation.1 | async-start | bytes 14155776 | tf_op jit(solution)/shard_map/all_gather | solution.py:21
  14.6 27.0 %copy-start.1 = (f32[384,2048]{1,0:T(8,128)}, f32[384,2048]{1,0:T(8,128)S(1)}, u32[]{:S(2)}) copy-start(f32[384,2048]{1,0:T(8,128)S(1)} %get-tuple-element.28) | copy-start | bytes 9437188
  40.1 1.5 copy-start.3
  40.1 1.6 copy-start.2
  41.6 146.9 %all-gather.3.cloned.1.call-start = ((), (), s32[]{:S(2)}) async-start(), calls=%async_computation | async-start | bytes 14155776 | tf_op jit(solution)/shard_map/all_gather | solution.py:20
  41.7 3.4 %copy-start.4 = (f32[96]{0:T(128)S(1)}, f32[96]{0:T(128)}, u32[]{:S(2)}) copy-start(f32[96]{0:T(128)} %param.10) | copy-start | bytes 1156
  41.7 3.4 %copy-start.5 = (f32[96]{0:T(128)S(1)}, f32[96]{0:T(128)}, u32[]{:S(2)}) copy-start(f32[96]{0:T(128)} %param.11) | copy-start | bytes 1156
  188.6 12.9 %copy-start = (bf16[3072,2048]{1,0:T(8,128)(2,1)S(1)}, bf16[3072,2048]{1,0:T(8,128)(2,1)}, u32[]{:S(2)}) copy-start(bf16[3072,2048]{1,0:T(8,128)(2,1)} %all-gather.5.cloned.1.call-done) | copy-start | bytes 37748740
Sparse Core Ops, SparseCore 0:
  41.7 72.3 all-gather.4
  116.6 71.9 all-gather.2
where the time goes:
time: 213 us
  waiting for transfers between devices  102 us (48%)
  blocking collectives  66.2 us (31%)
  local copies, waits for them, and re-layouts  18 us (8%)
  between operations  14.1 us (7%)
  other arithmetic  12.2 us (6%)
    all_gather x1, waiting for transfers between devices, body(): lax.all_gather(narrow_gate, 'shard', axis=0, tiled=True)  74.5 us
    unnamed x1, blocking collectives  40.7 us
    all_gather x1, waiting for transfers between devices, body(): lax.all_gather(narrow_up, 'shard', axis=0, tiled=True)  28 us
    pmax x1, blocking collectives, body(): lax.pmax((jnp.max(jnp.abs(whole_gate), axis=0), jnp.max(jnp.abs(whole_up)...  25.5 us
    unnamed x16, local copies, waits for them, and re-layouts  18 us
    reduce_max x1, other arithmetic, body(): jnp.max(jnp.abs(whole_up), axis=0)  7.37 us
  transfers between devices with their start and end apart: 2, of which 2 were waited for; matrix products, arithmetic and copies ran while one was open for 2% of the time, Pallas kernels for 0%

commit v1 on v0

v1 whole, which is shorter than its diff:
```python
import functools
import math

import jax
import jax.numpy as jnp
from jax import lax
from jax.experimental import pallas as pl
from jax.experimental.pallas import tpu as pltpu
from jax.sharding import PartitionSpec as P

MESH = pl.DeviceIdType.MESH
keep_rate = 0.7


def grid_of(n_shard):
    chips = n_shard // 2
    nx = math.isqrt(chips)
    while chips % nx:
        nx -= 1
    return chips // nx, nx


def kernel(
    n_shard, n_model, ny, nx, pieces, strip,
    weight_gate, smooth_gate, weight_up, smooth_up, norm_train, norm_step,
    serve_gate, serve_up, factor_gate, factor_up, norm_all, whole_gate, whole_up,
    weights, smooths, peaks,
    load_sem, peak_send, peak_recv, norm_send, norm_recv, row_send, row_recv,
    x_send, y_send, pair_send, ring_recv, pair_recv,
):
    me = lax.axis_index("shard")
    col = lax.axis_index("model")
    core = lax.rem(me, 2)
    chip = me // 2
    xpos, ypos = lax.rem(chip, nx), chip // nx
    x_next = (ypos * nx + lax.rem(xpos + 1, nx)) * 2 + core
    y_next = (lax.rem(ypos + 1, ny) * nx + xpos) * 2 + core
    pair = chip * 2 + (1 - core)
    rows, cols = whole_gate.shape
    part = rows // pieces
    serves, wholes, factors = (serve_gate, serve_up), (whole_gate, whole_up), (factor_gate, factor_up)

    loads = {}
    for unit, (w_ref, s_ref) in enumerate(((weight_gate, smooth_gate), (weight_up, smooth_up))):
        for k in range(pieces):
            span = pl.ds(k * part, part)
            for which, (src, dst) in enumerate(((w_ref, weights), (s_ref, smooths))):
                copy = pltpu.make_async_copy(src.at[span], dst.at[unit, span], load_sem.at[unit, k, which])
                copy.start()
                loads[unit, k, which] = copy

    barrier = pltpu.get_barrier_semaphore()
    for d in range(1, n_shard):
        pl.semaphore_signal(barrier, inc=1, device_id=(lax.rem(me + d, n_shard), col), device_id_type=MESH)
    for d in range(1, n_model):
        pl.semaphore_signal(barrier, inc=1, device_id=(me, lax.rem(col + d, n_model)), device_id_type=MESH)

    per = norm_train.shape[1]
    norm_all[me, col, :, 0:per] = norm_train[...] + norm_step[...]

    def average(unit):
        top = jnp.zeros((8, cols), jnp.float32)
        for k in range(pieces):
            loads[unit, k, 0].wait()
            loads[unit, k, 1].wait()

            def step(i, top):
                span = pl.ds(pl.multiple_of(k * part + i * 8, 8), 8)
                value = keep_rate * smooths[unit, span, :] + (1.0 - keep_rate) * weights[unit, span, :]
                wholes[unit][span, :] = value
                return jnp.maximum(top, jnp.abs(value))

            top = lax.fori_loop(0, part // 8, step, top)
        peaks[unit, me] = jnp.max(top, axis=0, keepdims=True)

    def send_peaks(unit):
        copies = []
        for d in range(1, n_shard):
            copy = pltpu.make_async_remote_copy(
                src_ref=peaks.at[unit, me], dst_ref=peaks.at[unit, me],
                send_sem=peak_send.at[unit, d - 1], recv_sem=peak_recv.at[unit, d - 1],
                device_id=(lax.rem(me + d, n_shard), col), device_id_type=MESH,
            )
            copy.start()
            copies.append(copy)
        return copies

    average(0)
    pl.semaphore_wait(barrier, n_shard + n_model - 2)
    peak_copies = [send_peaks(0)]
    norm_copies = []
    for d in range(1, n_model):
        copy = pltpu.make_async_remote_copy(
            src_ref=norm_all.at[me, col], dst_ref=norm_all.at[me, col],
            send_sem=norm_send.at[d - 1], recv_sem=norm_recv.at[d - 1],
            device_id=(me, lax.rem(col + d, n_model)), device_id_type=MESH,
        )
        copy.start()
        norm_copies.append(copy)
    average(1)
    peak_copies.append(send_peaks(1))

    def place(dy, dx, k):
        owner = (lax.rem(ypos - dy + ny, ny) * nx + lax.rem(xpos - dx + nx, nx)) * 2
        return owner, k

    def piece_of(unit, dy, dx, k, side):
        owner = (lax.rem(ypos - dy + ny, ny) * nx + lax.rem(xpos - dx + nx, nx)) * 2 + side
        return serves[unit].at[pl.ds(pl.multiple_of(owner * rows + k * part, part), part)]

    sent = []

    def start(unit, dy, dx, k, device, send_sem, recv_sem):
        ref = piece_of(unit, dy, dx, k, core)
        copy = pltpu.make_async_remote_copy(
            src_ref=ref, dst_ref=ref, send_sem=send_sem, recv_sem=recv_sem,
            device_id=(device, col), device_id_type=MESH,
        )
        copy.start()
        sent.append(copy)

    def forward(unit, dy, dx, k):
        to_x = dx < nx - 1 and (unit == 1 or dy == 0)
        to_y = dy < ny - 1 and (unit == 0 or dx == 0)
        if to_x:
            start(unit, dy, dx, k, x_next, x_send.at[unit, dy, dx, k], ring_recv.at[unit, dy, dx + 1, k])
        if to_y:
            start(unit, dy, dx, k, y_next, y_send.at[unit, dy, dx, k], ring_recv.at[unit, dy + 1, dx, k])
        start(unit, dy, dx, k, pair, pair_send.at[unit, dy, dx, k], pair_recv.at[unit, dy, dx, k])

    def arrived(unit, dy, dx, k):
        ref = piece_of(unit, dy, dx, k, core)
        pltpu.make_async_copy(ref, ref, ring_recv.at[unit, dy, dx, k]).wait()

    for unit in range(2):
        for copy in peak_copies[unit]:
            copy.wait_recv()
        factor = peaks[unit, 0]
        for d in range(1, n_shard):
            factor = jnp.maximum(factor, peaks[unit, d])
        factors[unit][...] = factor
        for k in range(pieces):

            def narrow(i, carry):
                at = k * part + i * strip
                value = wholes[unit][pl.ds(pl.multiple_of(at, strip), strip), :] / factors[unit][...]
                serves[unit][pl.ds(pl.multiple_of(me * rows + at, strip), strip), :] = value.astype(jnp.bfloat16)
                return carry

            lax.fori_loop(0, part // strip, narrow, 0)
            if k:
                forward(unit, 0, 0, k - 1)
        if unit == 0:
            last = (0, 0, 0, pieces - 1)
        if unit == 0:
            for copy in norm_copies:
                copy.wait_recv()
            forward(*last)
    row_copies = []
    for d in range(1, n_shard):
        copy = pltpu.make_async_remote_copy(
            src_ref=norm_all.at[me], dst_ref=norm_all.at[me],
            send_sem=row_send.at[d - 1], recv_sem=row_recv.at[d - 1],
            device_id=(lax.rem(me + d, n_shard), col), device_id_type=MESH,
        )
        copy.start()
        row_copies.append(copy)
    forward(1, 0, 0, pieces - 1)

    for distance in range(1, ny + nx - 1):
        for unit in range(2):
            for k in range(pieces):
                for dy in range(ny):
                    dx = distance - dy
                    if 0 <= dx < nx:
                        arrived(unit, dy, dx, k)
                        forward(unit, dy, dx, k)

    for unit in range(2):
        for dy in range(ny):
            for dx in range(nx):
                for k in range(pieces):
                    ref = piece_of(unit, dy, dx, k, 1 - core)
                    pltpu.make_async_copy(ref, ref, pair_recv.at[unit, dy, dx, k]).wait()
    for copy in sent + peak_copies[0] + peak_copies[1] + norm_copies + row_copies:
        copy.wait_send()
    for copy in row_copies:
        copy.wait_recv()


def store_kernel(*refs):
    half = len(refs) // 2
    copies = []
    for i, (src, dst) in enumerate(zip(refs[:half], refs[half:-1])):
        copy = pltpu.make_async_copy(src, dst, refs[-1].at[i])
        copy.start()
        copies.append(copy)
    for copy in copies:
        copy.wait()


def store(arrays):
    hbm = pl.BlockSpec(memory_space=pltpu.HBM)
    return pl.pallas_call(
        store_kernel,
        out_shape=tuple(pltpu.HBM(a.shape, a.dtype) for a in arrays),
        in_specs=[pl.BlockSpec(memory_space=pltpu.VMEM)] * len(arrays),
        out_specs=(hbm,) * len(arrays),
        scratch_shapes=[pltpu.SemaphoreType.DMA((len(arrays),))],
        compiler_params=pltpu.CompilerParams(vmem_limit_bytes=1024 * 1024),
    )(*(pltpu.with_memory_space_constraint(a, pltpu.VMEM) for a in arrays))


def solution(mesh):
    n_shard, n_model = mesh.shape["shard"], mesh.shape["model"]
    ny, nx = grid_of(n_shard)
    pieces = max(1, 16 // (ny * nx))

    def body(weight_gate, smooth_gate, weight_up, smooth_up, norm_train, norm_step):
        rows, cols = weight_gate.shape
        per = norm_train.shape[0]
        wide = -(-per // 128) * 128
        vmem = pl.BlockSpec(memory_space=pltpu.VMEM)
        hbm = pl.BlockSpec(memory_space=pltpu.HBM)
        dma = pltpu.SemaphoreType.DMA
        full = (n_shard * rows, cols)
        landed = pl.pallas_call(
            functools.partial(kernel, n_shard, n_model, ny, nx, pieces, 16),
            out_shape=(
                pltpu.VMEM(full, jnp.bfloat16),
                pltpu.VMEM(full, jnp.bfloat16),
                pltpu.VMEM((1, cols), jnp.float32),
                pltpu.VMEM((1, cols), jnp.float32),
                pltpu.VMEM((n_shard, n_model, 1, wide), jnp.float32),
                pltpu.VMEM((rows, cols), jnp.float32),
                pltpu.VMEM((rows, cols), jnp.float32),
            ),
            in_specs=[hbm, hbm, hbm, hbm, vmem, vmem],
            out_specs=(vmem,) * 7,
            scratch_shapes=[
                pltpu.VMEM((2, rows, cols), jnp.float32),
                pltpu.VMEM((2, rows, cols), jnp.float32),
                pltpu.VMEM((2, n_shard, 1, cols), jnp.float32),
                dma((2, pieces, 2)),
                dma((2, n_shard)),
                dma((2, n_shard)),
                dma((n_model,)),
                dma((n_model,)),
                dma((n_shard,)),
                dma((n_shard,)),
                dma((2, ny, nx, pieces)),
                dma((2, ny, nx, pieces)),
                dma((2, ny, nx, pieces)),
                dma((2, ny, nx, pieces)),
                dma((2, ny, nx, pieces)),
            ],
            compiler_params=pltpu.CompilerParams(
                collective_id=0, has_side_effects=True, vmem_limit_bytes=20 * 1024 * 1024
            ),
        )(
            *(pltpu.with_memory_space_constraint(a, pltpu.HBM) for a in (weight_gate, smooth_gate, weight_up, smooth_up)),
            norm_train[None], norm_step[None],
        )
        serve_gate, serve_up, factor_gate, factor_up, norm_all, whole_gate, whole_up = store(landed)
        serve_norm = norm_all[:, :, 0, :per].reshape(-1).astype(jnp.bfloat16)
        return (
            serve_gate, serve_up, factor_gate.reshape(-1), factor_up.reshape(-1),
            serve_norm, whole_gate, whole_up,
        )

    in_specs = (P("shard", "model"),) * 4 + (P(("shard", "model")),) * 2
    out_specs = (
        P(None, "model"),
        P(None, "model"),
        P("model"),
        P("model"),
        P(),
        P("shard", "model"),
        P("shard", "model"),
    )
    return jax.shard_map(body, mesh=mesh, in_specs=in_specs, out_specs=out_specs, check_vma=False)
```

time: 213 us -> 133 us (0.62)
  Pallas kernels: 0 us -> 129 us
  waiting for transfers between devices: 102 us -> 0 us
  blocking collectives: 66.2 us -> 0 us
  local copies, waits for them, and re-layouts: 18 us -> 2.76 us
  between operations: 14.1 us -> 0.66 us
  other arithmetic: 12.2 us -> 0 us
    pallas_call x0 -> x2, Pallas kernels: none -> 129 us  [the longest x1 118 us: body(): pl.pallas_call(functools.partial(kernel, n_shard, n_model, ny, nx, pieces...]
    all_gather x2 -> x0, waiting for transfers between devices: 102 us -> none  [the longest x1 74.5 us: body(): lax.all_gather(narrow_gate, 'shard', axis=0, tiled=True)]
    unnamed x1 -> x0, blocking collectives: 40.7 us -> none
    pmax x1 -> x0, blocking collectives: 25.5 us -> none  [body(): lax.pmax((jnp.max(jnp.abs(whole_gate), axis=0), jnp.max(jnp.abs(whole_up)...]
    unnamed x16 -> x4, local copies, waits for them, and re-layouts: 18 us -> 1.3 us
    reduce_max x1 -> x0, other arithmetic: 7.37 us -> none  [body(): jnp.max(jnp.abs(whole_up), axis=0)]
    convert_element_type x3 -> x0, other arithmetic: 4.85 us -> none  [the longest x1 3.37 us: body(): (whole_gate / factor_gate).astype(jnp.bfloat16)]
  transfers between devices with their start and end apart: 2 -> 0, of which waited for: 2 -> 0; matrix products, arithmetic and copies ran while one was open for 2% -> 0% of each run, Pallas kernels for 0% -> 0%
where the time goes in v1:
time: 133 us; the launch traced here: 132 us
  Pallas kernels  129 us (97%)
  local copies, waits for them, and re-layouts  2.76 us (2%)
    pallas_call x1, Pallas kernels, body(): pl.pallas_call(functools.partial(kernel, n_shard, n_model, ny, nx, pieces...  118 us
    pallas_call x1, Pallas kernels, store(): pl.pallas_call(store_kernel, out_shape=tuple((pltpu.HBM(a.shape, a.dtype)...  10.6 us

profile of v1, /device:TPU:0, one launch (start us, length us, event | category | flops | bytes accessed | tf_op | source)
XLA Modules:
  0.0 132.4 jit_solution(8242613838227110461)
XLA Ops:
  0.6 0.0 copy-start
  0.6 0.6 copy-done
  1.3 0.0 copy-start.1
  1.3 0.7 copy-done.1
  1.9 118.4 %shard_map.117 = (bf16[3072,2048]{1,0:T(8,128)(2,1)S(1)}, bf16[3072,2048]{1,0:T(8,128)(2,1)S(1)}, f32[1,2048]{1,0:T(1,128)S(1)}, f32[1,2048]{1,0:T(1,128)S(1)}, ...) custom-call(f32[384,2048]{1,0:T(8,128)} %weight_gate.1, f32[384,2048]{1,0:T(8,128)} %smooth_gate.1, ...), custom_call_target="tpu_custom_call" | custom-call | tf_op jit(solution)/shard_map/pallas_call | solution.py:227
  120.3 10.6 %shard_map.118 = (bf16[3072,2048]{1,0:T(8,128)(2,1)}, bf16[3072,2048]{1,0:T(8,128)(2,1)}, f32[1,2048]{1,0:T(1,128)}, f32[1,2048]{1,0:T(1,128)}, f32[8,4,1,128]{3...) custom-call(bf16[3072,2048]{1,0:T(8,128)(2,1)S(1)} %get-tuple-element.21.refs_0_, ...), custom_call_target="tpu_custom_call" | custom-call | tf_op jit(solution)/shard_map/pallas_call | solution.py:204
  130.9 0.8 fusion
  131.7 0.7 convert_element_type.4
Async XLA Ops:
  0.6 0.7 copy-start
  1.3 0.7 copy-start.1

commit v2 on v1

v2 whole, which is shorter than its diff:
```python
import functools
import math

import jax
import jax.numpy as jnp
from jax import lax
from jax.experimental import pallas as pl
from jax.experimental.pallas import tpu as pltpu
from jax.sharding import PartitionSpec as P

MESH = pl.DeviceIdType.MESH
keep_rate = 0.7


def grid_of(n_shard):
    chips = n_shard // 2
    nx = math.isqrt(chips)
    while chips % nx:
        nx -= 1
    return chips // nx, nx


def kernel(
    n_shard, n_model, ny, nx, pieces,
    weight_gate, smooth_gate, weight_up, smooth_up, norm_train, norm_step,
    serve_gate, serve_up, factor_gate, factor_up, norm_all, whole_gate, whole_up,
    weights, smooths, peaks, norm_in,
    load_sem, norm_load, peak_send, peak_recv, norm_send, norm_recv, row_send, row_recv,
    x_send, y_send, pair_send, ring_recv, pair_recv,
):
    me = lax.axis_index("shard")
    col = lax.axis_index("model")
    core = lax.rem(me, 2)
    chip = me // 2
    xpos, ypos = lax.rem(chip, nx), chip // nx
    x_next = (ypos * nx + lax.rem(xpos + 1, nx)) * 2 + core
    y_next = (lax.rem(ypos + 1, ny) * nx + xpos) * 2 + core
    pair = chip * 2 + (1 - core)
    rows, cols = whole_gate.shape
    part = cols // pieces
    serves, wholes, factors = (serve_gate, serve_up), (whole_gate, whole_up), (factor_gate, factor_up)

    norm_loads = [
        pltpu.make_async_copy(src, norm_in.at[i], norm_load.at[i]) for i, src in enumerate((norm_train, norm_step))
    ]
    for copy in norm_loads:
        copy.start()
    loads = {}
    for unit, (w_ref, s_ref) in enumerate(((weight_gate, smooth_gate), (weight_up, smooth_up))):
        for k in sorted(range(pieces), key=lambda k: k % max(1, pieces // 2)):
            span = pl.ds(k * part, part)
            for which, (src, dst) in enumerate(((w_ref, weights), (s_ref, smooths))):
                copy = pltpu.make_async_copy(src.at[:, span], dst.at[unit, :, span], load_sem.at[unit, k, which])
                copy.start()
                loads[unit, k, which] = copy

    barrier = pltpu.get_barrier_semaphore()
    for d in range(1, n_shard):
        pl.semaphore_signal(barrier, inc=1, device_id=(lax.rem(me + d, n_shard), col), device_id_type=MESH)
    for d in range(1, n_model):
        pl.semaphore_signal(barrier, inc=1, device_id=(me, lax.rem(col + d, n_model)), device_id_type=MESH)

    per = norm_train.shape[1]
    for copy in norm_loads:
        copy.wait()
    norm_all[me, col, :, 0:per] = norm_in[0] + norm_in[1]

    def average(unit, k):
        for which in range(2):
            loads[unit, k, which].wait()
        across = pl.ds(k * part, part)

        def step(i, top):
            span = pl.ds(pl.multiple_of(i * 8, 8), 8)
            value = keep_rate * smooths[unit, span, across] + (1.0 - keep_rate) * weights[unit, span, across]
            wholes[unit][span, across] = value
            return jnp.maximum(top, jnp.abs(value))

        top = lax.fori_loop(0, rows // 8, step, jnp.zeros((8, part), jnp.float32), unroll=4)
        peaks[unit, k, me] = jnp.max(top, axis=0, keepdims=True)

    def send_peaks(unit, k):
        copies = []
        for d in range(1, n_shard):
            copy = pltpu.make_async_remote_copy(
                src_ref=peaks.at[unit, k, me], dst_ref=peaks.at[unit, k, me],
                send_sem=peak_send.at[unit, k, d - 1], recv_sem=peak_recv.at[unit, k, d - 1],
                device_id=(lax.rem(me + d, n_shard), col), device_id_type=MESH,
            )
            copy.start()
            copies.append(copy)
        return copies

    order = [(unit, k) for unit in range(2) for k in sorted(range(pieces), key=lambda k: k % max(1, pieces // 2))]
    peak_copies = {}
    norm_copies = []
    for n, (unit, k) in enumerate(order):
        average(unit, k)
        if n == 0:
            pl.semaphore_wait(barrier, n_shard + n_model - 2)
        peak_copies[unit, k] = send_peaks(unit, k)
    for d in range(1, n_model):
        copy = pltpu.make_async_remote_copy(
            src_ref=norm_all.at[me, col], dst_ref=norm_all.at[me, col],
            send_sem=norm_send.at[d - 1], recv_sem=norm_recv.at[d - 1],
            device_id=(me, lax.rem(col + d, n_model)), device_id_type=MESH,
        )
        copy.start()
        norm_copies.append(copy)

    def piece_of(unit, dy, dx, k, side):
        owner = (lax.rem(ypos - dy + ny, ny) * nx + lax.rem(xpos - dx + nx, nx)) * 2 + side
        return serves[unit].at[k, pl.ds(pl.multiple_of(owner * rows, rows), rows)]

    sent = []

    def start(unit, dy, dx, k, device, send_sem, recv_sem):
        ref = piece_of(unit, dy, dx, k, core)
        copy = pltpu.make_async_remote_copy(
            src_ref=ref, dst_ref=ref, send_sem=send_sem, recv_sem=recv_sem,
            device_id=(device, col), device_id_type=MESH,
        )
        copy.start()
        sent.append(copy)

    def along_x_first(unit, k):
        return 2 * k < pieces if pieces > 1 else unit == 0

    def to_x(unit, dy, dx, k):
        if dx < nx - 1 and (dy == 0 or not along_x_first(unit, k)):
            start(unit, dy, dx, k, x_next, x_send.at[unit, dy, dx, k], ring_recv.at[unit, dy, dx + 1, k])

    def to_y(unit, dy, dx, k):
        if dy < ny - 1 and (dx == 0 or along_x_first(unit, k)):
            start(unit, dy, dx, k, y_next, y_send.at[unit, dy, dx, k], ring_recv.at[unit, dy + 1, dx, k])

    def to_pair(unit, dy, dx, k):
        start(unit, dy, dx, k, pair, pair_send.at[unit, dy, dx, k], pair_recv.at[unit, dy, dx, k])

    def arrived(unit, dy, dx, k):
        ref = piece_of(unit, dy, dx, k, core)
        pltpu.make_async_copy(ref, ref, ring_recv.at[unit, dy, dx, k]).wait()

    def first_way(unit, k):
        (to_x if along_x_first(unit, k) else to_y)(unit, 0, 0, k)

    before = None
    for unit, k in order:
        across = pl.ds(k * part, part)
        for copy in peak_copies[unit, k]:
            copy.wait_recv()
        factor = peaks[unit, k, 0]
        for d in range(1, n_shard):
            factor = jnp.maximum(factor, peaks[unit, k, d])
        factors[unit][:, across] = factor
        if before:
            first_way(*before)

        def narrow(i, carry):
            at = i * 16
            value = wholes[unit][pl.ds(pl.multiple_of(at, 16), 16), across] / factors[unit][:, across]
            serves[unit][k, pl.ds(pl.multiple_of(me * rows + at, 16), 16)] = value.astype(jnp.bfloat16)
            return carry

        lax.fori_loop(0, rows // 16, narrow, 0, unroll=2)
        before = (unit, k)
    for copy in norm_copies:
        copy.wait_recv()
    row_copies = []
    for d in range(1, n_shard):
        copy = pltpu.make_async_remote_copy(
            src_ref=norm_all.at[me], dst_ref=norm_all.at[me],
            send_sem=row_send.at[d - 1], recv_sem=row_recv.at[d - 1],
            device_id=(lax.rem(me + d, n_shard), col), device_id_type=MESH,
        )
        copy.start()
        row_copies.append(copy)
    first_way(*before)
    for unit, k in order:
        (to_y if along_x_first(unit, k) else to_x)(unit, 0, 0, k)
    for unit, k in order:
        to_pair(unit, 0, 0, k)

    for distance in range(1, ny + nx - 1):
        for own_way in (True, False):
            for unit, k in order:
                for dy in range(ny):
                    dx = distance - dy
                    straight = (dy if along_x_first(unit, k) else dx) == 0
                    if 0 <= dx < nx and straight == own_way:
                        arrived(unit, dy, dx, k)
                        to_x(unit, dy, dx, k)
                        to_y(unit, dy, dx, k)
                        to_pair(unit, dy, dx, k)

    for unit in range(2):
        for dy in range(ny):
            for dx in range(nx):
                for k in range(pieces):
                    ref = piece_of(unit, dy, dx, k, 1 - core)
                    pltpu.make_async_copy(ref, ref, pair_recv.at[unit, dy, dx, k]).wait()
    for copy in sent + sum(peak_copies.values(), []) + norm_copies + row_copies:
        copy.wait_send()
    for copy in row_copies:
        copy.wait_recv()


def store_kernel(count, *refs):
    copies = []

    def move(src, dst):
        copies.append(pltpu.make_async_copy(src, dst, refs[-1].at[len(copies)]))
        copies[-1].start()

    for src, dst in zip(refs[:count], refs[count:-1]):
        if src.shape == dst.shape:
            move(src, dst)
            continue
        pieces, rows, part = src.shape
        for k in range(pieces):
            for half in range(2):
                span = pl.ds(half * (rows // 2), rows // 2)
                move(src.at[k, span], dst.at[span, pl.ds(k * part, part)])
    for copy in copies:
        copy.wait()


def store(arrays, shapes):
    hbm = pl.BlockSpec(memory_space=pltpu.HBM)
    return pl.pallas_call(
        functools.partial(store_kernel, len(arrays)),
        out_shape=tuple(pltpu.HBM(shape, a.dtype) for a, shape in zip(arrays, shapes)),
        in_specs=[pl.BlockSpec(memory_space=pltpu.VMEM)] * len(arrays),
        out_specs=(hbm,) * len(arrays),
        scratch_shapes=[pltpu.SemaphoreType.DMA((len(arrays) + 4 * arrays[0].shape[0],))],
        compiler_params=pltpu.CompilerParams(vmem_limit_bytes=1024 * 1024),
    )(*(pltpu.with_memory_space_constraint(a, pltpu.VMEM) for a in arrays))


def solution(mesh):
    n_shard, n_model = mesh.shape["shard"], mesh.shape["model"]
    ny, nx = grid_of(n_shard)

    def body(weight_gate, smooth_gate, weight_up, smooth_up, norm_train, norm_step):
        rows, cols = weight_gate.shape
        per = norm_train.shape[0]
        pieces = math.gcd(max(1, 16 // (ny * nx)), cols // 128)
        wide = -(-per // 128) * 128
        vmem = pl.BlockSpec(memory_space=pltpu.VMEM)
        hbm = pl.BlockSpec(memory_space=pltpu.HBM)
        dma = pltpu.SemaphoreType.DMA
        full = (pieces, n_shard * rows, cols // pieces)
        landed = pl.pallas_call(
            functools.partial(kernel, n_shard, n_model, ny, nx, pieces),
            out_shape=(
                pltpu.VMEM(full, jnp.bfloat16),
                pltpu.VMEM(full, jnp.bfloat16),
                pltpu.VMEM((1, cols), jnp.float32),
                pltpu.VMEM((1, cols), jnp.float32),
                pltpu.VMEM((n_shard, n_model, 1, wide), jnp.float32),
                pltpu.VMEM((rows, cols), jnp.float32),
                pltpu.VMEM((rows, cols), jnp.float32),
            ),
            in_specs=[hbm] * 6,
            out_specs=(vmem,) * 7,
            scratch_shapes=[
                pltpu.VMEM((2, rows, cols), jnp.float32),
                pltpu.VMEM((2, rows, cols), jnp.float32),
                pltpu.VMEM((2, pieces, n_shard, 1, cols // pieces), jnp.float32),
                pltpu.VMEM((2, 1, per), jnp.float32),
                dma((2, pieces, 2)),
                dma((2,)),
                dma((2, pieces, n_shard)),
                dma((2, pieces, n_shard)),
                dma((n_model,)),
                dma((n_model,)),
                dma((n_shard,)),
                dma((n_shard,)),
                dma((2, ny, nx, pieces)),
                dma((2, ny, nx, pieces)),
                dma((2, ny, nx, pieces)),
                dma((2, ny, nx, pieces)),
                dma((2, ny, nx, pieces)),
            ],
            compiler_params=pltpu.CompilerParams(
                collective_id=0, has_side_effects=True, vmem_limit_bytes=20 * 1024 * 1024
            ),
        )(
            *(
                pltpu.with_memory_space_constraint(a, pltpu.HBM)
                for a in (weight_gate, smooth_gate, weight_up, smooth_up, norm_train[None], norm_step[None])
            ),
        )
        serve_gate, serve_up, factor_gate, factor_up, norm_all, whole_gate, whole_up = store(
            landed, ((n_shard * rows, cols),) * 2 + tuple(a.shape for a in landed[2:])
        )
        serve_norm = norm_all[:, :, 0, :per].reshape(-1).astype(jnp.bfloat16)
        return (
            serve_gate, serve_up, factor_gate.reshape(-1), factor_up.reshape(-1),
            serve_norm, whole_gate, whole_up,
        )

    in_specs = (P("shard", "model"),) * 4 + (P(("shard", "model")),) * 2
    out_specs = (
        P(None, "model"),
        P(None, "model"),
        P("model"),
        P("model"),
        P(),
        P("shard", "model"),
        P("shard", "model"),
    )
    return jax.shard_map(body, mesh=mesh, in_specs=in_specs, out_specs=out_specs, check_vma=False)
```

time: 133 us -> 131 us (0.985)
  no operation moved by 1% of the time
where the time goes in v2:
time: 131 us
  Pallas kernels  129 us (98%)
  local copies, waits for them, and re-layouts  1.45 us (1%)
    pallas_call x1, Pallas kernels, body(): pl.pallas_call(functools.partial(kernel, n_shard, n_model, ny, nx, pieces...  118 us
    pallas_call x1, Pallas kernels, store(): pl.pallas_call(functools.partial(store_kernel, len(arrays)), out_shape=tu...  10.5 us

profile of v2, /device:TPU:0, one launch (start us, length us, event | category | flops | bytes accessed | tf_op | source)
XLA Modules:
  0.0 131.1 jit_solution(16203629532192800367)
XLA Ops:
  0.6 118.4 %shard_map.117 = (bf16[4,3072,512]{2,1,0:T(8,128)(2,1)S(1)}, bf16[4,3072,512]{2,1,0:T(8,128)(2,1)S(1)}, f32[1,2048]{1,0:T(1,128)S(1)}, f32[1,2048]{1,0:T(1,128)S...) custom-call(f32[384,2048]{1,0:T(8,128)} %weight_gate.1, ...), custom_call_target="tpu_custom_call" | custom-call | tf_op jit(solution)/shard_map/pallas_call | solution.py:253
  119.1 10.5 %shard_map.118 = (bf16[3072,2048]{1,0:T(8,128)(2,1)}, bf16[3072,2048]{1,0:T(8,128)(2,1)}, f32[1,2048]{1,0:T(1,128)}, f32[1,2048]{1,0:T(1,128)}, f32[8,4,1,128]{3...) custom-call(bf16[4,3072,512]{2,1,0:T(8,128)(2,1)S(1)} %get-tuple-element.21.refs_0_, ...), custom_call_target="tpu_custom_call" | custom-call | tf_op jit(solution)/shard_map/pallas_call | solution.py:230
  129.6 0.8 fusion
  130.4 0.7 convert_element_type.4
